TPU v7x, 128 devices: a whole 4x4x4 slice. The times are simulated.
128 devices in a mesh: rows: 32 (over y, x, core), model: 4 (over z).
Axes of the slice: x: 4, y: 4, z: 4, core: 2. Of those that a mesh axis runs over, the one named last changes fastest.
Arguments:
- weight_gate: bfloat16 [2048, 8192], P('rows', 'model'), may hold values from -0.125 to 0.125
- low_gate: bfloat16 [2048, 64], P('rows'), may hold values from -0.125 to 0.125
- high_gate: bfloat16 [64, 8192], P(None, 'model'), may hold values from -0.75 to 0.75
- weight_up: bfloat16 [2048, 8192], P('rows', 'model'), may hold values from -0.125 to 0.125
- low_up: bfloat16 [2048, 64], P('rows'), may hold values from -0.125 to 0.125
- high_up: bfloat16 [64, 8192], P(None, 'model'), may hold values from -0.75 to 0.75
- weight_down: bfloat16 [8192, 2048], P('model', 'rows'), may hold values from -0.0625 to 0.0625
- low_down: bfloat16 [8192, 64], P('model'), may hold values from -0.0625 to 0.0625
- high_down: bfloat16 [64, 2048], P(None, 'rows'), may hold values from -0.75 to 0.75
- norm_train: float32 [2048], P(('rows', 'model')), may hold values from 0.25 to 1.75
- norm_step: float32 [2048], P(('rows', 'model')), may hold values from -0.3 to 0.3
Outputs:
- final_gate: bfloat16 [8192, 2048], P('model')
- final_up: bfloat16 [8192, 2048], P('model')
- final_down: bfloat16 [2048, 8192], P(None, 'model')
- serve_norm: bfloat16 [2048], replicated
All inputs are finite; a program needn't handle non-finite values.
Results may differ from a plain program's by a relative error of at most 0.001.
Values may be sent and summed in bfloat16 or wider, within the bound.
A program may use at most 192 MiB of HBM per device.

v0:
```python
import jax
import jax.numpy as jnp
from jax import lax
from jax.sharding import Mesh
from jax.sharding import PartitionSpec as P

ROWS = ("rows_0", "rows_1", "rows_2")
ROWS_MODEL = ("rows_0", "rows_1", "rows_2", "model")


mix_rate = 0.5


def turned_gather(arrays, axis, dims):
    turned = [jnp.moveaxis(a, dim, 0) for a, dim in zip(arrays, dims)]
    both = jnp.concatenate([t.reshape(len(t), -1) for t in turned], axis=1)
    result, at, finished = (lax.all_gather(both, axis, axis=0, tiled=True), 0, [])
    for t, dim in zip(turned, dims):
        section = result[:, at : at + t[0].size].reshape(-1, *t.shape[1:])
        finished.append(jnp.moveaxis(section, 0, dim))
        at += t[0].size
    return tuple(finished)


def in_order(tiles, dim):
    dims = list(tiles.shape[1:])
    dims[dim] *= tiles.shape[0]
    return jnp.moveaxis(tiles, 0, dim).reshape(dims)


def stacked_from(array, axes, turns):
    tiles = array
    for k in turns:
        tiles = lax.all_gather(tiles, axes[k])
    done = turns[::-1]
    back = [done.index(k) for k in range(len(axes))]
    tiles = tiles.transpose(*back, *range(len(axes), tiles.ndim))
    return tiles.reshape(-1, *array.shape)


def gathered_by_axis(array, axes, turns, dim):
    return in_order(stacked_from(array, axes, turns), dim)


def local(
    weight_gate,
    low_gate,
    high_gate,
    weight_up,
    low_up,
    high_up,
    weight_down,
    low_down,
    high_down,
    norm_train,
    norm_step,
):
    result_gate = weight_gate.astype(jnp.float32) + mix_rate * jnp.dot(
        low_gate, high_gate, preferred_element_type=jnp.float32
    )
    result_up = weight_up.astype(jnp.float32) + mix_rate * jnp.dot(
        low_up, high_up, preferred_element_type=jnp.float32
    )
    result_down = weight_down.astype(jnp.float32) + mix_rate * jnp.dot(
        low_down, high_down, preferred_element_type=jnp.float32
    )
    narrow_gate, narrow_up, narrow_down = (
        result_gate.astype(jnp.bfloat16),
        result_up.astype(jnp.bfloat16),
        result_down.astype(jnp.bfloat16),
    )
    final_gate, final_up, final_down = turned_gather(
        (narrow_gate, narrow_up, narrow_down), ROWS, (0, 0, 1)
    )
    final_gate, final_up, final_down = (final_gate.T, final_up.T, final_down.T)
    serve_norm = gathered_by_axis(
        (norm_train + norm_step).astype(jnp.bfloat16), ROWS_MODEL, (0, 1, 3, 2), 0
    )
    return (final_gate, final_up, final_down, serve_norm)


def solution(mesh):
    split = Mesh(
        mesh.devices.reshape(4, 4, 2, mesh.shape["model"]), ("rows_0", "rows_1", "rows_2", "model")
    )
    placed = (
        P(ROWS, "model"),
        P(ROWS, None),
        P(None, "model"),
        P(ROWS, "model"),
        P(ROWS, None),
        P(None, "model"),
        P("model", ROWS),
        P("model", None),
        P(None, ROWS),
        P(ROWS_MODEL),
        P(ROWS_MODEL),
    )
    return jax.shard_map(
        local,
        mesh=split,
        in_specs=placed,
        out_specs=(P("model", None), P("model", None), P(None, "model"), P()),
        check_vma=False,
    )
```

profile of v0, /device:TPU:1, one launch (start us, length us, event | category | flops | bytes accessed | tf_op | source)
XLA Modules:
  0.0 156.6 jit_solution(8086940729364175655)
XLA Ops:
  7.2 0.0 copy-start
  7.2 0.0 all-gather.7.cloned.1.call-start
  7.2 0.9 copy-done
  8.1 1.2 fusion.4
  9.3 1.3 fusion.5
  10.6 1.3 fusion.6
  11.9 0.9 pad_maximum_fusion
  12.8 0.0 all-gather.7.cloned.1.call-update
  12.9 1.2 dynamic-slice
  14.8 0.7 add_convert_fusion
  15.4 0.2 dynamic-update-slice
  15.6 9.5 %all-reduce = bf16[64]{0:T(256)(128)(2,1)S(1)} all-reduce(bf16[64]{0:T(256)(128)(2,1)S(1)} %dynamic-update-slice), channel_id=2, replica_groups=mesh['rows_0'=4,'rows_1'=4,'rows_2'=2,'model'=4] {'rows_0'}, use_global_device_ids=true, to_apply=%add | all-reduce | flops 64 | bytes 256
  25.2 0.1 reshape.15
  25.2 8.7 %all-gather.4 = bf16[4,4,16]{2,1,0:T(4,128)(2,1)S(1)} all-gather(bf16[1,4,16]{2,1,0:T(4,128)(2,1)S(1)} %reshape.15), channel_id=3, replica_groups=mesh['rows_0'=4,'rows_1'=4,'rows_2'=2,'model'=4] {'rows_1'}, dimensions={0}, use_global_device_ids=true | all-gather | bytes 640 | tf_op jit(solution)/shard_map/all_gather | solution.py:34
  33.9 11.1 %all-gather.2 = bf16[16,4,16]{2,1,0:T(4,128)(2,1)S(1)} all-gather(bf16[4,4,16]{2,1,0:T(4,128)(2,1)S(1)} %all-gather.4), channel_id=4, replica_groups=mesh['rows_0'=4,'rows_1'=4,'rows_2'=2,'model'=4] {'model'}, dimensions={0}, use_global_device_ids=true | all-gather | bytes 2560 | tf_op jit(solution)/shard_map/all_gather | solution.py:34
  45.0 7.4 %all-gather.3 = bf16[8,4,4,16]{3,2,1,0:T(4,128)(2,1)S(1)} all-gather(bf16[4,4,4,16]{3,2,1,0:T(4,128)(2,1)S(1)} %bitcast.20), channel_id=5, replica_groups=mesh['rows_0'=4,'rows_1'=4,'rows_2'=2,'model'=4] {'rows_2'}, dimensions={0}, use_global_device_ids=true | all-gather | bytes 6144 | tf_op jit(solution)/shard_map/all_gather | solution.py:34
  52.4 0.7 reshape_reshape.3
  53.1 55.3 %all-gather.7.cloned.1.call-done = bf16[2048,6144]{1,0:T(8,128)(2,1)} async-done(((bf16[64,6144]{1,0:T(8,128)(2,1)}), bf16[2048,6144]{1,0:T(8,128)(2,1)}) %all-gather.7.cloned.1.call-update) | async-done | bytes 25165840 | tf_op jit(solution)/shard_map/all_gather | solution.py:17
  108.4 16.9 %fusion.7 = (bf16[2048,2048]{1,0:T(8,128)(2,1)}, bf16[2048,2048]{0,1:T(8,128)(2,1)}, bf16[2048,2048]{0,1:T(8,128)(2,1)}) fusion(bf16[2048,6144]{1,0:T(8,128)(2,1)} %all-gather.7.cloned.1.call-done), kind=kLoop, calls=%fused_computation.15 | loop fusion | bytes 50331648 | tf_op jit(solution)/shard_map/slice | solution.py:19
  125.3 12.2 %copy.21 = bf16[2048,2048]{1,0:T(8,128)(2,1)} copy(bf16[2048,2048]{0,1:T(8,128)(2,1)} %get-tuple-element.18) | data formatting | bytes 16777216
  137.5 0.0 copy-start.1
  137.5 12.3 %copy.22 = bf16[2048,2048]{1,0:T(8,128)(2,1)} copy(bf16[2048,2048]{0,1:T(8,128)(2,1)} %get-tuple-element.17) | data formatting | bytes 16777216
  149.8 0.0 copy-done.1
  (2 shorter events, 0.0 us)
Async XLA Ops:
  7.2 1.0 copy-start
  7.2 101.2 %all-gather.7.cloned.1.call-start = ((), (), s32[]{:S(2)}) async-start(), calls=%async_computation | async-start | bytes 25952256 | tf_op jit(solution)/shard_map/all_gather | solution.py:17
  137.5 12.3 %copy-start.1 = (bf16[64,2048]{1,0:T(8,128)(2,1)S(1)}, bf16[64,2048]{1,0:T(8,128)(2,1)}, u32[]{:S(2)}) copy-start(bf16[64,2048]{1,0:T(8,128)(2,1)} %param.16) | copy-start | bytes 786436
Sparse Core Ops, SparseCore 0:
  13.0 95.3 all-gather.6
where the time goes:
time: 157 us
  waiting for transfers between devices  55.3 us (35%)
  local copies, waits for them, and re-layouts  44.6 us (28%)
  blocking collectives  36.6 us (23%)
  between operations  14.7 us (9%)
  matrix products  3.75 us (2%)
  other arithmetic  1.61 us (1%)
    all_gather x1, waiting for transfers between devices, turned_gather(): lax.all_gather(both, axis, axis=0, tiled=True)  55.3 us
    all_gather x3, blocking collectives, stacked_from(): tiles = lax.all_gather(tiles, axes[k])  27.1 us
    unnamed x10, local copies, waits for them, and re-layouts  26.9 us
    slice x1, local copies, waits for them, and re-layouts, turned_gather(): section = result[:, at:at + t[0].size].reshape(-1, *t.shape[1:])  16.9 us
    unnamed x1, blocking collectives  9.52 us
  transfers between devices with their start and end apart: 1, of which 1 were waited for; matrix products, arithmetic and copies ran while one was open for 2% of the time, Pallas kernels for 0%

commit v1 on v0

v1 whole, which is shorter than its diff:
```python
import functools

import jax
import jax.numpy as jnp
from jax import lax
from jax.experimental import pallas as pl
from jax.experimental.pallas import tpu as pltpu
from jax.sharding import Mesh
from jax.sharding import PartitionSpec as P

ROWS = ("rows_0", "rows_1", "rows_2")
ROWS_MODEL = ("rows_0", "rows_1", "rows_2", "model")
MESH = pl.DeviceIdType.MESH

mix_rate = 0.5

TREES = (("x", 1), ("x", -1), ("y", 1), ("y", -1))
DOWN, GATE, UP = 0, 1, 2


def tree_slots(sign):
    steps = (0, sign, -sign, 2 * sign)
    hops = {0: 0, sign: 1, -sign: 1, 2 * sign: 2}
    slots = [(a, b) for a in steps for b in steps if (a, b) != (0, 0)]
    return sorted(slots, key=lambda s: (hops[s[0]] + hops[s[1]], hops[s[1]]))


def onward(a, b, sign):
    places = []
    if b == 0:
        if a == 0:
            places += [(sign, 0), (-sign, 0)]
        elif a == sign:
            places += [(2 * sign, 0)]
        places += [(a, sign), (a, -sign)]
    elif b == sign:
        places += [(a, 2 * sign)]
    return places


def slot_number(a, b):
    return (a % 4) * 4 + b % 4


def gather_kernel(
    wd_in, ld_in, hd_in, wg_in, lg_in, hg_in, wu_in, lu_in, hu_in, train_in, step_in,
    down, gate, up, norm,
    wd, ld, hd, wg, lg, hg, wu, lu, hu, train, step, row, part, zrow,
    in_sem, part_send, part_recv, send_sem, side_send, side_recv, recv_sem,
    n_send, n_recv,
):
    y, x, k, z = (lax.axis_index(n) for n in ROWS_MODEL)
    other = 1 - k
    chip = y * 4 + x

    def toward(axis, by):
        if axis == "x":
            return {"rows_1": lax.rem(x + by + 4, 4)}
        if axis == "y":
            return {"rows_0": lax.rem(y + by + 4, 4)}
        return {"model": lax.rem(z + by + 4, 4)}

    partner = {"rows_2": other}

    half = pl.ds(pl.multiple_of(k * 1024, 1024), 1024)
    half_other = pl.ds(pl.multiple_of(other * 1024, 1024), 1024)
    mine = pl.ds(pl.multiple_of(k * 64, 64), 64)
    reads = [
        pltpu.make_async_copy(s, d, in_sem.at[i])
        for i, (s, d) in enumerate(
            [
                (wd_in, wd), (ld_in, ld), (hd_in, hd),
                (wg_in.at[:, half], wg.at[mine]), (lg_in, lg.at[mine]), (hg_in.at[:, half], hg),
                (wu_in.at[:, half], wu.at[mine]), (lu_in, lu.at[mine]), (hu_in.at[:, half], hu),
                (train_in, train), (step_in, step),
            ]
        )
    ]
    for r in reads:
        r.start()

    barrier = pltpu.get_barrier_semaphore()
    peers = [partner] + [toward(axis, by) for axis in "xyz" for by in (1, -1)]
    for p in peers:
        pl.semaphore_signal(barrier, inc=1, device_id=p, device_id_type=MESH)

    lane = lax.broadcasted_iota(jnp.int32, (1, 128), 1)
    first = k * 64 + z * 16
    reads[9].wait()
    reads[10].wait()
    own = jnp.zeros((1, 128), jnp.float32)
    for i in range(16):
        own = jnp.where(lane == first + i, train[i] + step[i], own)
    row[...] = own

    pl.semaphore_wait(barrier, len(peers))

    def to_partner(i, src, dst):
        return pltpu.make_async_remote_copy(
            src_ref=src, dst_ref=dst, send_sem=part_send.at[i], recv_sem=part_recv.at[i],
            device_id=partner, device_id_type=MESH,
        )

    swaps = [
        to_partner(0, wg_in.at[:, half_other], wg.at[mine]),
        to_partner(1, lg_in, lg.at[mine]),
        to_partner(2, wu_in.at[:, half_other], wu.at[mine]),
        to_partner(3, lu_in, lu.at[mine]),
        to_partner(4, row, part),
    ]
    for s in swaps:
        s.start()

    def piece(arr, t, c):
        if arr == DOWN:
            return down.at[c, k, pl.ds(16 * t, 16), :]
        ref = gate if arr == GATE else up
        return ref.at[k, t, :, pl.ds(pl.multiple_of(c * 128, 128), 128)]

    def origin(t, a, b):
        dx, dy = (a, b) if TREES[t][0] == "x" else (b, a)
        return lax.rem(y - dy + 4, 4) * 4 + lax.rem(x - dx + 4, 4)

    def copy_on(arr, t, a, b, c, na, nb):
        first_axis = TREES[t][0]
        second_axis = "y" if first_axis == "x" else "x"
        sign = TREES[t][1]
        if na != a:
            axis, by = first_axis, (-sign if na == -sign else sign)
        else:
            axis, by = second_axis, (-sign if nb == -sign else sign)
        ref = piece(arr, t, c)
        return pltpu.make_async_remote_copy(
            src_ref=ref, dst_ref=ref, send_sem=send_sem.at[arr],
            recv_sem=recv_sem.at[(arr * 4 + t) * 16 + slot_number(na, nb)],
            device_id=toward(axis, by), device_id_type=MESH,
        )

    def send_on(arr, t, a, b, c):
        for na, nb in onward(a, b, TREES[t][1]):
            copy_on(arr, t, a, b, c, na, nb).start()
        ref = piece(arr, t, c)
        pltpu.make_async_remote_copy(
            src_ref=ref, dst_ref=ref, send_sem=side_send.at[arr], recv_sem=side_recv.at[arr],
            device_id=partner, device_id_type=MESH,
        ).start()

    def arrive(arr, t, a, b):
        c = origin(t, a, b)
        ref = piece(arr, t, c)
        pltpu.make_async_remote_copy(
            src_ref=ref, dst_ref=ref, send_sem=send_sem.at[arr],
            recv_sem=recv_sem.at[(arr * 4 + t) * 16 + slot_number(a, b)],
            device_id=partner, device_id_type=MESH,
        ).wait_recv()
        send_on(arr, t, a, b, c)

    for i in range(3):
        reads[i].wait()
    mix = lax.dot_general(hd[...], ld[...], (((0,), (0,)), ((), ())), preferred_element_type=jnp.float32)
    down[chip, k] = (wd[...].astype(jnp.float32) + mix_rate * mix).astype(jnp.bfloat16)
    swaps[4].wait()
    zrow[0] = row[...] + part[...]
    for t in range(4):
        send_on(DOWN, t, 0, 0, chip)

    def turned(ref, w, low, high):
        for t in range(4):
            cols = pl.ds(256 * t, 256)
            mix = jnp.dot(low[...], high[:, cols], preferred_element_type=jnp.float32)
            full = w[:, cols].astype(jnp.float32) + mix_rate * mix
            ref[k, t, :, pl.ds(pl.multiple_of(chip * 128, 128), 128)] = full.T.astype(jnp.bfloat16)

    for i in (3, 4, 5):
        reads[i].wait()
    swaps[0].wait()
    swaps[1].wait()
    turned(gate, wg, lg, hg)

    def norm_copy(src, dst, slot, to):
        return pltpu.make_async_remote_copy(
            src_ref=src, dst_ref=dst, send_sem=n_send.at[slot], recv_sem=n_recv.at[slot],
            device_id=to, device_id_type=MESH,
        )

    z_up = norm_copy(zrow.at[0], zrow.at[1], 16, toward("z", 1))
    z_down = norm_copy(zrow.at[0], zrow.at[2], 17, toward("z", -1))
    z_far = norm_copy(zrow.at[1], zrow.at[3], 18, toward("z", 1))
    z_up.start()
    z_down.start()

    for t in range(4):
        send_on(GATE, t, 0, 0, chip)

    for i in (6, 7, 8):
        reads[i].wait()
    swaps[2].wait()
    swaps[3].wait()
    turned(up, wu, lu, hu)
    z_up.wait()
    z_far.start()

    def each(arr):
        order = tree_slots(1)
        return [(arr, t, TREES[t][1] * a, TREES[t][1] * b) for a, b in order for t in range(4)]

    for e in each(DOWN):
        arrive(*e)

    z_down.wait()
    z_far.wait()
    norm[chip] = zrow[0] + zrow[1] + zrow[2] + zrow[3]

    for t in range(4):
        send_on(UP, t, 0, 0, chip)

    def norm_on(a, b, c):
        sign = TREES[0][1]
        for na, nb in onward(a, b, sign):
            if na != a:
                to = toward("x", -sign if na == -sign else sign)
            else:
                to = toward("y", -sign if nb == -sign else sign)
            norm_copy(norm.at[c], norm.at[c], slot_number(na, nb), to).start()

    def norm_arrive(a, b):
        c = origin(0, a, b)
        norm_copy(norm.at[c], norm.at[c], slot_number(a, b), partner).wait_recv()
        norm_on(a, b, c)

    norm_on(0, 0, chip)
    for e in each(GATE):
        arrive(*e)
    for a, b in tree_slots(TREES[0][1]):
        norm_arrive(a, b)
    for e in each(UP):
        arrive(*e)

    for a, b in tree_slots(TREES[0][1]):
        norm_copy(norm.at[0], norm.at[0], slot_number(a, b), partner).wait_send()

    def drain(arr, ref, part_send_ref, other_half, own_half):
        pltpu.make_async_copy(part_send_ref, part_send_ref, send_sem.at[arr]).wait()
        pltpu.make_async_copy(own_half, own_half, side_send.at[arr]).wait()
        pltpu.make_async_copy(other_half, other_half, side_recv.at[arr]).wait()

    drain(DOWN, down, down.at[pl.ds(0, 15), k], down.at[:, other], down.at[:, k])
    drain(GATE, gate, gate.at[k, :, :, pl.ds(0, 1920)], gate.at[other], gate.at[k])
    drain(UP, up, up.at[k, :, :, pl.ds(0, 1920)], up.at[other], up.at[k])


def write_kernel(down, gate, up, norm, down_out, gate_out, up_out, norm_out, sem):
    copies = []
    for n, (src, dst) in enumerate([(gate, gate_out), (up, up_out)]):
        for h in range(2):
            for t in range(4):
                copies.append((src.at[h, t], dst.at[h, t]))
    for q in range(8):
        rows = pl.ds(2 * q, 2)
        copies.append((down.at[rows], down_out.at[rows]))
    copies = [pltpu.make_async_copy(s, d, sem.at[i]) for i, (s, d) in enumerate(copies)]
    for c in copies:
        c.start()
    norm_out[...] = norm[...].reshape(16, 128).astype(jnp.bfloat16)
    for c in copies:
        c.wait()


def local(
    weight_gate, low_gate, high_gate, weight_up, low_up, high_up,
    weight_down, low_down, high_down, norm_train, norm_step,
):
    bf16, f32 = jnp.bfloat16, jnp.float32
    hbm = pl.BlockSpec(memory_space=pltpu.HBM)
    vmem = pl.BlockSpec(memory_space=pltpu.VMEM)
    dma = pltpu.SemaphoreType.DMA
    down, gate, up, norm = pl.pallas_call(
        gather_kernel,
        out_shape=(
            pltpu.VMEM((16, 2, 64, 2048), bf16),
            pltpu.VMEM((2, 4, 256, 2048), bf16),
            pltpu.VMEM((2, 4, 256, 2048), bf16),
            pltpu.VMEM((16, 1, 128), f32),
        ),
        in_specs=[hbm] * 11,
        out_specs=(vmem,) * 4,
        scratch_shapes=[
            pltpu.VMEM((64, 2048), bf16), pltpu.VMEM((64, 2048), bf16), pltpu.VMEM((64, 64), bf16),
            pltpu.VMEM((128, 1024), bf16), pltpu.VMEM((128, 64), bf16), pltpu.VMEM((64, 1024), bf16),
            pltpu.VMEM((128, 1024), bf16), pltpu.VMEM((128, 64), bf16), pltpu.VMEM((64, 1024), bf16),
            pltpu.SMEM((16,), f32), pltpu.SMEM((16,), f32),
            pltpu.VMEM((1, 128), f32), pltpu.VMEM((1, 128), f32), pltpu.VMEM((4, 1, 128), f32),
            dma((11,)), dma((5,)), dma((5,)), dma((3,)), dma((3,)), dma((3,)), dma((192,)),
            dma((19,)), dma((19,)),
        ],
        compiler_params=pltpu.CompilerParams(
            collective_id=0, has_side_effects=True, vmem_limit_bytes=8 << 20
        ),
        name="gather",
    )(*(
        pltpu.with_memory_space_constraint(a, pltpu.HBM)
        for a in (
            weight_down.T, low_down.T, high_down, weight_gate, low_gate, high_gate,
            weight_up, low_up, high_up, norm_train, norm_step,
        )
    ))
    down, gate, up, norm = pl.pallas_call(
        write_kernel,
        out_shape=(
            jax.ShapeDtypeStruct((16, 2, 64, 2048), bf16),
            jax.ShapeDtypeStruct((2, 4, 256, 2048), bf16),
            jax.ShapeDtypeStruct((2, 4, 256, 2048), bf16),
            jax.ShapeDtypeStruct((16, 128), bf16),
        ),
        in_specs=[vmem] * 4,
        out_specs=(hbm, hbm, hbm, vmem),
        scratch_shapes=[dma((24,))],
        compiler_params=pltpu.CompilerParams(vmem_limit_bytes=4 << 20),
        name="write",
    )(down, gate, up, norm)
    return gate.reshape(2048, 2048), up.reshape(2048, 2048), down.reshape(2048, 2048), norm.reshape(2048)


def solution(mesh):
    split = Mesh(
        mesh.devices.reshape(4, 4, 2, mesh.shape["model"]), ROWS_MODEL
    )
    placed = (
        P(ROWS, "model"),
        P(ROWS, None),
        P(None, "model"),
        P(ROWS, "model"),
        P(ROWS, None),
        P(None, "model"),
        P("model", ROWS),
        P("model", None),
        P(None, ROWS),
        P(ROWS_MODEL),
        P(ROWS_MODEL),
    )
    return jax.shard_map(
        local,
        mesh=split,
        in_specs=placed,
        out_specs=(P("model", None), P("model", None), P(None, "model"), P()),
        check_vma=False,
    )
```

time: 157 us -> 99.4 us (0.63)
  Pallas kernels: 0 us -> 98.6 us
  waiting for transfers between devices: 55.3 us -> 0 us
  local copies, waits for them, and re-layouts: 44.6 us -> 0 us
  blocking collectives: 36.6 us -> 0 us
  between operations: 14.7 us -> 0.64 us
  matrix products: 3.75 us -> 0 us
  other arithmetic: 1.61 us -> 0 us
    pallas_call x0 -> x2, Pallas kernels: none -> 98.6 us  [the longest x1 89.5 us: local(): pl.pallas_call(gather_kernel, out_shape=(pltpu.VMEM((16, 2, 64, 2048), bf...]
    all_gather x1 -> x0, waiting for transfers between devices: 55.3 us -> none  [turned_gather(): lax.all_gather(both, axis, axis=0, tiled=True)]
    all_gather x3 -> x0, blocking collectives: 27.1 us -> none  [stacked_from(): tiles = lax.all_gather(tiles, axes[k])]
    unnamed x10 -> x0, local copies, waits for them, and re-layouts: 26.9 us -> none
    slice x1 -> x0, local copies, waits for them, and re-layouts: 16.9 us -> none  [turned_gather(): section = result[:, at:at + t[0].size].reshape(-1, *t.shape[1:])]
    unnamed x1 -> x0, blocking collectives: 9.52 us -> none
    dot_general x3 -> x0, matrix products: 3.75 us -> none  [the longest x1 1.32 us: local(): jnp.dot(low_down, high_down, preferred_element_type=jnp.float32)]
  transfers between devices with their start and end apart: 1 -> 0, of which waited for: 1 -> 0; matrix products, arithmetic and copies ran while one was open for 2% -> 0% of each run, Pallas kernels for 0% -> 0%
where the time goes in v1:
time: 99.4 us; the launch traced here: 99.3 us
  Pallas kernels  98.6 us (99%)
    pallas_call x1, Pallas kernels, local(): pl.pallas_call(gather_kernel, out_shape=(pltpu.VMEM((16, 2, 64, 2048), bf...  89.5 us
    pallas_call x1, Pallas kernels, local(): pl.pallas_call(write_kernel, out_shape=(jax.ShapeDtypeStruct((16, 2, 64,...  9.15 us

profile of v1, /device:TPU:1, one launch (start us, length us, event | category | flops | bytes accessed | tf_op | source)
XLA Modules:
  0.0 99.3 jit_solution(6372434293901420888)
XLA Ops:
  0.6 89.5 %gather.1 = (bf16[16,2,64,2048]{3,2,1,0:T(8,128)(2,1)S(1)}, bf16[2,4,256,2048]{3,2,1,0:T(8,128)(2,1)S(1)}, bf16[2,4,256,2048]{3,2,1,0:T(8,128)(2,1)S(1)}, f32[16,1,128]{2,1,0:T(1,128)S(1)}) custom-call(bf16[64,2048]{1,0:T(8,128)(2,1)} %bitcast.6, bf16[64,2048]{1,0:T(8,128)(2,1)} %bitcast.7, bf16[64,64]{1,0:T(8,128)(2,1)} %hd_in.1, bf16[64,2048]{1,0:T(8,128)(2,1)} %wg_in.1, ...), custom_call_target="tpu_custom_call" | custom-call | tf_op jit(solution)/shard_map/gather/pallas_call | solution.py:277
  90.1 9.1 %write.1 = (bf16[16,2,64,2048]{3,2,1,0:T(8,128)(2,1)}, bf16[2,4,256,2048]{3,2,1,0:T(8,128)(2,1)}, bf16[2,4,256,2048]{3,2,1,0:T(8,128)(2,1)}, bf16[16,128]{1,0:T(8,128)(2,1)}) custom-call(bf16[16,2,64,2048]{3,2,1,0:T(8,128)(2,1)S(1)} %get-tuple-element.12.down, bf16[2,4,256,2048]{3,2,1,0:T(8,128)(2,1)S(1)} %get-tuple-element.13.gate, ...), custom_call_target="tpu_custom_call" | custom-call | tf_op jit(solution)/shard_map/write/pallas_call | solution.py:307

commit v2 on v1

--- a/solution.py
+++ b/solution.py
@@ -197,22 +197,17 @@
     swaps[2].wait()
     swaps[3].wait()
     turned(up, wu, lu, hu)
+    for t in range(4):
+        send_on(UP, t, 0, 0, chip)
     z_up.wait()
     z_far.start()
 
-    def each(arr):
-        order = tree_slots(1)
-        return [(arr, t, TREES[t][1] * a, TREES[t][1] * b) for a, b in order for t in range(4)]
-
-    for e in each(DOWN):
-        arrive(*e)
-
-    z_down.wait()
-    z_far.wait()
-    norm[chip] = zrow[0] + zrow[1] + zrow[2] + zrow[3]
-
-    for t in range(4):
-        send_on(UP, t, 0, 0, chip)
+    def level(hops):
+        signs = [(a, b) for a, b in tree_slots(1) if abs(a) + abs(b) == hops]
+        return [
+            (arr, t, TREES[t][1] * a, TREES[t][1] * b)
+            for arr in (DOWN, GATE, UP) for a, b in signs for t in range(4)
+        ]
 
     def norm_on(a, b, c):
         sign = TREES[0][1]
@@ -228,13 +223,19 @@
         norm_copy(norm.at[c], norm.at[c], slot_number(a, b), partner).wait_recv()
         norm_on(a, b, c)
 
+    for e in level(1):
+        arrive(*e)
+    z_down.wait()
+    z_far.wait()
+    norm[chip] = zrow[0] + zrow[1] + zrow[2] + zrow[3]
     norm_on(0, 0, chip)
-    for e in each(GATE):
-        arrive(*e)
-    for a, b in tree_slots(TREES[0][1]):
-        norm_arrive(a, b)
-    for e in each(UP):
-        arrive(*e)
+    for hops in (2, 3, 4):
+        for e in level(hops):
+            arrive(*e)
+        for a, b in tree_slots(TREES[0][1]):
+            if abs(a) + abs(b) == hops - 1:
+                norm_arrive(a, b)
+    norm_arrive(2, 2)
 
     for a, b in tree_slots(TREES[0][1]):
         norm_copy(norm.at[0], norm.at[0], slot_number(a, b), partner).wait_send()

time: 99.4 us -> 89.8 us (0.903)
  Pallas kernels: 98.6 us -> 88.8 us
    pallas_call x1, Pallas kernels: 89.5 us -> 79.7 us  [local(): pl.pallas_call(gather_kernel, out_shape=(pltpu.VMEM((16, 2, 64, 2048), bf...]
where the time goes in v2:
time: 89.8 us; the launch traced here: 89.5 us
  Pallas kernels  88.8 us (99%)
    pallas_call x1, Pallas kernels, local(): pl.pallas_call(gather_kernel, out_shape=(pltpu.VMEM((16, 2, 64, 2048), bf...  79.7 us
    pallas_call x1, Pallas kernels, local(): pl.pallas_call(write_kernel, out_shape=(jax.ShapeDtypeStruct((16, 2, 64,...  9.15 us

profile of v2, /device:TPU:1, one launch (start us, length us, event | category | flops | bytes accessed | tf_op | source)
XLA Modules:
  0.0 89.5 jit_solution(11922406170547923793)
XLA Ops:
  0.6 79.7 %gather.1 = (bf16[16,2,64,2048]{3,2,1,0:T(8,128)(2,1)S(1)}, bf16[2,4,256,2048]{3,2,1,0:T(8,128)(2,1)S(1)}, bf16[2,4,256,2048]{3,2,1,0:T(8,128)(2,1)S(1)}, f32[16,1,128]{2,1,0:T(1,128)S(1)}) custom-call(bf16[64,2048]{1,0:T(8,128)(2,1)} %bitcast.6, bf16[64,2048]{1,0:T(8,128)(2,1)} %bitcast.7, bf16[64,64]{1,0:T(8,128)(2,1)} %hd_in.1, bf16[64,2048]{1,0:T(8,128)(2,1)} %wg_in.1, ...), custom_call_target="tpu_custom_call" | custom-call | tf_op jit(solution)/shard_map/gather/pallas_call | solution.py:278
  80.3 9.1 %write.1 = (bf16[16,2,64,2048]{3,2,1,0:T(8,128)(2,1)}, bf16[2,4,256,2048]{3,2,1,0:T(8,128)(2,1)}, bf16[2,4,256,2048]{3,2,1,0:T(8,128)(2,1)}, bf16[16,128]{1,0:T(8,128)(2,1)}) custom-call(bf16[16,2,64,2048]{3,2,1,0:T(8,128)(2,1)S(1)} %get-tuple-element.12.down, bf16[2,4,256,2048]{3,2,1,0:T(8,128)(2,1)S(1)} %get-tuple-element.13.gate, ...), custom_call_target="tpu_custom_call" | custom-call | tf_op jit(solution)/shard_map/write/pallas_call | solution.py:308

commit v3 on v2

--- a/solution.py
+++ b/solution.py
@@ -42,16 +42,21 @@
     return (a % 4) * 4 + b % 4
 
 
+WAYS = (("x", 1), ("x", -1), ("y", 1), ("y", -1), ("x", 2), ("y", 2))
+BACK = (1, 0, 3, 2, 4, 5)
+
+
 def gather_kernel(
     wd_in, ld_in, hd_in, wg_in, lg_in, hg_in, wu_in, lu_in, hu_in, train_in, step_in,
-    down, gate, up, norm,
-    wd, ld, hd, wg, lg, hg, wu, lu, hu, train, step, row, part, zrow,
+    down, gate, up, norm_out,
+    wd, ld, hd, wg, lg, hg, wu, lu, hu, train, step, norm, part, total, below, above, tosend,
     in_sem, part_send, part_recv, send_sem, side_send, side_recv, recv_sem,
-    n_send, n_recv,
+    n_send, n_recv, ready,
 ):
     y, x, k, z = (lax.axis_index(n) for n in ROWS_MODEL)
     other = 1 - k
     chip = y * 4 + x
+    place = {"x": x, "y": y}
 
     def toward(axis, by):
         if axis == "x":
@@ -78,22 +83,45 @@
     ]
     for r in reads:
         r.start()
+    below[...] = jnp.zeros_like(below)
+    above[...] = jnp.zeros_like(above)
+
+    def later(way):
+        axis, by = WAYS[way]
+        p = place[axis]
+        return (p == 0) | (p == 3) if by == -1 else p < 2
 
     barrier = pltpu.get_barrier_semaphore()
-    peers = [partner] + [toward(axis, by) for axis in "xyz" for by in (1, -1)]
-    for p in peers:
-        pl.semaphore_signal(barrier, inc=1, device_id=p, device_id_type=MESH)
-
-    lane = lax.broadcasted_iota(jnp.int32, (1, 128), 1)
-    first = k * 64 + z * 16
-    reads[9].wait()
-    reads[10].wait()
-    own = jnp.zeros((1, 128), jnp.float32)
-    for i in range(16):
-        own = jnp.where(lane == first + i, train[i] + step[i], own)
-    row[...] = own
-
-    pl.semaphore_wait(barrier, len(peers))
+    pl.semaphore_signal(barrier, inc=1, device_id=partner, device_id_type=MESH)
+    for w in range(6):
+        @pl.when(later(w))
+        def _(w=w):
+            pl.semaphore_signal(barrier, inc=1, device_id=toward(*WAYS[w]), device_id_type=MESH)
+
+    @pl.when(z < 3)
+    def _():
+        pl.semaphore_signal(barrier, inc=1, device_id=toward("z", 1), device_id_type=MESH)
+
+    one, nil = jnp.int32(1), jnp.int32(0)
+    greetings = 1 + jnp.where(z > 0, one, nil)
+    for w in range(6):
+        greetings = greetings + jnp.where(later(w), nil, one)
+    pl.semaphore_wait(barrier, greetings)
+    for w in range(6):
+        @pl.when(jnp.logical_not(later(w)))
+        def _(w=w):
+            pl.semaphore_signal(
+                ready.at[BACK[w]], inc=1, device_id=toward(*WAYS[w]), device_id_type=MESH
+            )
+
+    @pl.when(z > 0)
+    def _():
+        pl.semaphore_signal(ready.at[6], inc=1, device_id=toward("z", -1), device_id_type=MESH)
+
+    def wait_ready(w):
+        @pl.when(later(w))
+        def _():
+            pl.semaphore_wait(ready.at[w], 1)
 
     def to_partner(i, src, dst):
         return pltpu.make_async_remote_copy(
@@ -106,10 +134,24 @@
         to_partner(1, lg_in, lg.at[mine]),
         to_partner(2, wu_in.at[:, half_other], wu.at[mine]),
         to_partner(3, lu_in, lu.at[mine]),
-        to_partner(4, row, part),
+        to_partner(4, norm, part),
     ]
-    for s in swaps:
+    for s in swaps[:4]:
         s.start()
+
+    reads[9].wait()
+    reads[10].wait()
+    lane = lax.broadcasted_iota(jnp.int32, (1, 128), 1)
+    first = k * 64 + z * 16
+    own = jnp.zeros((1, 128), jnp.float32)
+    for i in range(16):
+        own = jnp.where(lane == first + i, train[i] + step[i], own)
+    norm[chip] = own
+
+    for i in range(3):
+        reads[i].wait()
+    mix = lax.dot_general(hd[...], ld[...], (((0,), (0,)), ((), ())), preferred_element_type=jnp.float32)
+    down[chip, k] = (wd[...].astype(jnp.float32) + mix_rate * mix).astype(jnp.bfloat16)
 
     def piece(arr, t, c):
         if arr == DOWN:
@@ -121,24 +163,28 @@
         dx, dy = (a, b) if TREES[t][0] == "x" else (b, a)
         return lax.rem(y - dy + 4, 4) * 4 + lax.rem(x - dx + 4, 4)
 
-    def copy_on(arr, t, a, b, c, na, nb):
-        first_axis = TREES[t][0]
+    def way_to(t, a, b, na, nb):
+        first_axis, sign = TREES[t]
         second_axis = "y" if first_axis == "x" else "x"
-        sign = TREES[t][1]
         if na != a:
-            axis, by = first_axis, (-sign if na == -sign else sign)
-        else:
-            axis, by = second_axis, (-sign if nb == -sign else sign)
+            return first_axis, (-sign if na == -sign else sign)
+        return second_axis, (-sign if nb == -sign else sign)
+
+    def copy_on(arr, t, c, na, nb, to):
         ref = piece(arr, t, c)
         return pltpu.make_async_remote_copy(
             src_ref=ref, dst_ref=ref, send_sem=send_sem.at[arr],
             recv_sem=recv_sem.at[(arr * 4 + t) * 16 + slot_number(na, nb)],
-            device_id=toward(axis, by), device_id_type=MESH,
-        )
-
-    def send_on(arr, t, a, b, c):
+            device_id=to, device_id_type=MESH,
+        )
+
+    def send_on(arr, t, a, b, c, only=None):
         for na, nb in onward(a, b, TREES[t][1]):
-            copy_on(arr, t, a, b, c, na, nb).start()
+            way = way_to(t, a, b, na, nb)
+            if only is None or way == only:
+                copy_on(arr, t, c, na, nb, toward(*way)).start()
+
+    def send_side(arr, t, c):
         ref = piece(arr, t, c)
         pltpu.make_async_remote_copy(
             src_ref=ref, dst_ref=ref, send_sem=side_send.at[arr], recv_sem=side_recv.at[arr],
@@ -147,22 +193,43 @@
 
     def arrive(arr, t, a, b):
         c = origin(t, a, b)
-        ref = piece(arr, t, c)
-        pltpu.make_async_remote_copy(
-            src_ref=ref, dst_ref=ref, send_sem=send_sem.at[arr],
-            recv_sem=recv_sem.at[(arr * 4 + t) * 16 + slot_number(a, b)],
-            device_id=partner, device_id_type=MESH,
-        ).wait_recv()
+        copy_on(arr, t, c, a, b, partner).wait_recv()
         send_on(arr, t, a, b, c)
-
-    for i in range(3):
-        reads[i].wait()
-    mix = lax.dot_general(hd[...], ld[...], (((0,), (0,)), ((), ())), preferred_element_type=jnp.float32)
-    down[chip, k] = (wd[...].astype(jnp.float32) + mix_rate * mix).astype(jnp.bfloat16)
-    swaps[4].wait()
-    zrow[0] = row[...] + part[...]
+        send_side(arr, t, c)
+
+    def row_copy(rows, w):
+        return pltpu.make_async_remote_copy(
+            src_ref=norm.at[rows], dst_ref=norm.at[rows], send_sem=n_send.at[w], recv_sem=n_recv.at[w],
+            device_id=toward(*WAYS[w]), device_id_type=MESH,
+        )
+
+    def row_from(w):
+        axis, by = WAYS[w]
+        if axis == "x":
+            return pl.ds(y * 4 + lax.rem(x - by + 4, 4), 1)
+        return pl.ds(lax.rem(y - by + 4, 4) * 4, 4)
+
+    def first_sends(w):
+        if w < 2:
+            row_copy(pl.ds(chip, 1), w).start()
+        for t in range(4):
+            send_on(DOWN, t, 0, 0, chip, only=WAYS[w])
+
+    for w in range(4):
+        @pl.when(jnp.logical_not(later(w)))
+        def _(w=w):
+            first_sends(w)
+
+    for w in range(4):
+        @pl.when(later(w))
+        def _(w=w):
+            pl.semaphore_wait(ready.at[w], 1)
+            first_sends(w)
+
+    wait_ready(4)
+    row_copy(pl.ds(chip, 1), 4).start()
     for t in range(4):
-        send_on(DOWN, t, 0, 0, chip)
+        send_side(DOWN, t, chip)
 
     def turned(ref, w, low, high):
         for t in range(4):
@@ -171,83 +238,113 @@
             full = w[:, cols].astype(jnp.float32) + mix_rate * mix
             ref[k, t, :, pl.ds(pl.multiple_of(chip * 128, 128), 128)] = full.T.astype(jnp.bfloat16)
 
-    for i in (3, 4, 5):
-        reads[i].wait()
-    swaps[0].wait()
-    swaps[1].wait()
-    turned(gate, wg, lg, hg)
-
-    def norm_copy(src, dst, slot, to):
+    for arr, ref, at, args in ((GATE, gate, 0, (wg, lg, hg)), (UP, up, 2, (wu, lu, hu))):
+        for i in range(3):
+            reads[3 + arr * 3 - 3 + i].wait()
+        swaps[at].wait()
+        swaps[at + 1].wait()
+        turned(ref, *args)
+        for t in range(4):
+            send_on(arr, t, 0, 0, chip)
+            send_side(arr, t, chip)
+
+    def rows_along_y():
+        for w in (0, 1, 4):
+            row_copy(row_from(w), w).wait_recv()
+        wait_ready(5)
+        for w in (2, 3, 5):
+            row_copy(pl.ds(y * 4, 4), w).start()
+
+    def rows_to_partner():
+        for w in (2, 3, 5):
+            row_copy(row_from(w), w).wait_recv()
+        swaps[4].start()
+
+    def rows_of_chip():
+        swaps[4].wait()
+        total[...] = norm[...] + part[...]
+
+    def z_copy(src, dst, i, by):
         return pltpu.make_async_remote_copy(
-            src_ref=src, dst_ref=dst, send_sem=n_send.at[slot], recv_sem=n_recv.at[slot],
-            device_id=to, device_id_type=MESH,
-        )
-
-    z_up = norm_copy(zrow.at[0], zrow.at[1], 16, toward("z", 1))
-    z_down = norm_copy(zrow.at[0], zrow.at[2], 17, toward("z", -1))
-    z_far = norm_copy(zrow.at[1], zrow.at[3], 18, toward("z", 1))
-    z_up.start()
-    z_down.start()
-
-    for t in range(4):
-        send_on(GATE, t, 0, 0, chip)
-
-    for i in (6, 7, 8):
-        reads[i].wait()
-    swaps[2].wait()
-    swaps[3].wait()
-    turned(up, wu, lu, hu)
-    for t in range(4):
-        send_on(UP, t, 0, 0, chip)
-    z_up.wait()
-    z_far.start()
+            src_ref=src, dst_ref=dst, send_sem=n_send.at[i], recv_sem=n_recv.at[i],
+            device_id=toward("z", by), device_id_type=MESH,
+        )
+
+    def z_ends():
+        @pl.when(z < 3)
+        def _():
+            pl.semaphore_wait(ready.at[6], 1)
+
+        @pl.when(z == 0)
+        def _():
+            z_copy(total, below, 6, 1).start()
+
+        @pl.when(z == 3)
+        def _():
+            z_copy(total, above, 7, -1).start()
+
+    def z_up_sum():
+        @pl.when(z > 0)
+        def _():
+            z_copy(total, below, 6, 1).wait_recv()
+        tosend[0] = total[...] + below[...]
+
+    def z_up_send():
+        @pl.when((z > 0) & (z < 3))
+        def _():
+            z_copy(tosend.at[0], below, 6, 1).start()
+
+    def z_down_sum():
+        @pl.when(z < 3)
+        def _():
+            z_copy(total, above, 7, -1).wait_recv()
+        tosend[1] = total[...] + above[...]
+
+    def z_down_send():
+        @pl.when((z > 0) & (z < 3))
+        def _():
+            z_copy(tosend.at[1], above, 7, -1).start()
+
+    def norm_end():
+        for w in range(6):
+            rows = pl.ds(0, 1) if WAYS[w][0] == "x" else pl.ds(0, 4)
+            row_copy(rows, w).wait_send()
+
+        @pl.when(z < 3)
+        def _():
+            z_copy(total, below, 6, 1).wait_send()
+
+        @pl.when(z > 0)
+        def _():
+            z_copy(total, above, 7, -1).wait_send()
+
+        norm_out[...] = tosend[0] + above[...]
 
     def level(hops):
-        signs = [(a, b) for a, b in tree_slots(1) if abs(a) + abs(b) == hops]
+        places = [(a, b) for a, b in tree_slots(1) if abs(a) + abs(b) == hops]
         return [
             (arr, t, TREES[t][1] * a, TREES[t][1] * b)
-            for arr in (DOWN, GATE, UP) for a, b in signs for t in range(4)
+            for arr in (DOWN, GATE, UP) for a, b in places for t in range(4)
         ]
 
-    def norm_on(a, b, c):
-        sign = TREES[0][1]
-        for na, nb in onward(a, b, sign):
-            if na != a:
-                to = toward("x", -sign if na == -sign else sign)
-            else:
-                to = toward("y", -sign if nb == -sign else sign)
-            norm_copy(norm.at[c], norm.at[c], slot_number(na, nb), to).start()
-
-    def norm_arrive(a, b):
-        c = origin(0, a, b)
-        norm_copy(norm.at[c], norm.at[c], slot_number(a, b), partner).wait_recv()
-        norm_on(a, b, c)
-
-    for e in level(1):
+    events = [e for hops in (1, 2, 3, 4) for e in level(hops)]
+    extra = {
+        0: rows_along_y, 48: rows_to_partner, 60: rows_of_chip, 72: z_ends,
+        96: z_up_sum, 108: z_up_send, 120: z_down_sum, 132: z_down_send, 150: norm_end,
+    }
+    for n, e in enumerate(events):
+        if n in extra:
+            extra[n]()
         arrive(*e)
-    z_down.wait()
-    z_far.wait()
-    norm[chip] = zrow[0] + zrow[1] + zrow[2] + zrow[3]
-    norm_on(0, 0, chip)
-    for hops in (2, 3, 4):
-        for e in level(hops):
-            arrive(*e)
-        for a, b in tree_slots(TREES[0][1]):
-            if abs(a) + abs(b) == hops - 1:
-                norm_arrive(a, b)
-    norm_arrive(2, 2)
-
-    for a, b in tree_slots(TREES[0][1]):
-        norm_copy(norm.at[0], norm.at[0], slot_number(a, b), partner).wait_send()
-
-    def drain(arr, ref, part_send_ref, other_half, own_half):
-        pltpu.make_async_copy(part_send_ref, part_send_ref, send_sem.at[arr]).wait()
+
+    def drain(arr, sent, other_half, own_half):
+        pltpu.make_async_copy(sent, sent, send_sem.at[arr]).wait()
         pltpu.make_async_copy(own_half, own_half, side_send.at[arr]).wait()
         pltpu.make_async_copy(other_half, other_half, side_recv.at[arr]).wait()
 
-    drain(DOWN, down, down.at[pl.ds(0, 15), k], down.at[:, other], down.at[:, k])
-    drain(GATE, gate, gate.at[k, :, :, pl.ds(0, 1920)], gate.at[other], gate.at[k])
-    drain(UP, up, up.at[k, :, :, pl.ds(0, 1920)], up.at[other], up.at[k])
+    drain(DOWN, down.at[pl.ds(0, 15), k], down.at[:, other], down.at[:, k])
+    drain(GATE, gate.at[k, :, :, pl.ds(0, 1920)], gate.at[other], gate.at[k])
+    drain(UP, up.at[k, :, :, pl.ds(0, 1920)], up.at[other], up.at[k])
 
 
 def write_kernel(down, gate, up, norm, down_out, gate_out, up_out, norm_out, sem):
@@ -275,6 +372,7 @@
     hbm = pl.BlockSpec(memory_space=pltpu.HBM)
     vmem = pl.BlockSpec(memory_space=pltpu.VMEM)
     dma = pltpu.SemaphoreType.DMA
+    rows = pltpu.VMEM((16, 1, 128), f32)
     down, gate, up, norm = pl.pallas_call(
         gather_kernel,
         out_shape=(
@@ -290,9 +388,9 @@
             pltpu.VMEM((128, 1024), bf16), pltpu.VMEM((128, 64), bf16), pltpu.VMEM((64, 1024), bf16),
             pltpu.VMEM((128, 1024), bf16), pltpu.VMEM((128, 64), bf16), pltpu.VMEM((64, 1024), bf16),
             pltpu.SMEM((16,), f32), pltpu.SMEM((16,), f32),
-            pltpu.VMEM((1, 128), f32), pltpu.VMEM((1, 128), f32), pltpu.VMEM((4, 1, 128), f32),
+            rows, rows, rows, rows, rows, pltpu.VMEM((2, 16, 1, 128), f32),
             dma((11,)), dma((5,)), dma((5,)), dma((3,)), dma((3,)), dma((3,)), dma((192,)),
-            dma((19,)), dma((19,)),
+            dma((8,)), dma((8,)), pltpu.SemaphoreType.REGULAR((7,)),
         ],
         compiler_params=pltpu.CompilerParams(
             collective_id=0, has_side_effects=True, vmem_limit_bytes=8 << 20

time: 89.8 us -> 83.1 us (0.925)
  Pallas kernels: 88.8 us -> 82.3 us
    pallas_call x1, Pallas kernels: 79.7 us -> 73.2 us  [local(): pl.pallas_call(gather_kernel, out_shape=(pltpu.VMEM((16, 2, 64, 2048), bf...]
where the time goes in v3:
time: 83.1 us; the launch traced here: 83 us
  Pallas kernels  82.3 us (99%)
    pallas_call x1, Pallas kernels, local(): pl.pallas_call(gather_kernel, out_shape=(pltpu.VMEM((16, 2, 64, 2048), bf...  73.2 us
    pallas_call x1, Pallas kernels, local(): pl.pallas_call(write_kernel, out_shape=(jax.ShapeDtypeStruct((16, 2, 64,...  9.15 us

profile of v3, /device:TPU:1, one launch (start us, length us, event | category | flops | bytes accessed | tf_op | source)
XLA Modules:
  0.0 83.0 jit_solution(10815826434190505781)
XLA Ops:
  0.6 73.2 %gather.1 = (bf16[16,2,64,2048]{3,2,1,0:T(8,128)(2,1)S(1)}, bf16[2,4,256,2048]{3,2,1,0:T(8,128)(2,1)S(1)}, bf16[2,4,256,2048]{3,2,1,0:T(8,128)(2,1)S(1)}, f32[16,1,128]{2,1,0:T(1,128)S(1)}) custom-call(bf16[64,2048]{1,0:T(8,128)(2,1)} %bitcast.6, bf16[64,2048]{1,0:T(8,128)(2,1)} %bitcast.7, bf16[64,64]{1,0:T(8,128)(2,1)} %hd_in.1, bf16[64,2048]{1,0:T(8,128)(2,1)} %wg_in.1, ...), custom_call_target="tpu_custom_call" | custom-call | tf_op jit(solution)/shard_map/gather/pallas_call | solution.py:376
  73.8 9.1 %write.1 = (bf16[16,2,64,2048]{3,2,1,0:T(8,128)(2,1)}, bf16[2,4,256,2048]{3,2,1,0:T(8,128)(2,1)}, bf16[2,4,256,2048]{3,2,1,0:T(8,128)(2,1)}, bf16[16,128]{1,0:T(8,128)(2,1)}) custom-call(bf16[16,2,64,2048]{3,2,1,0:T(8,128)(2,1)S(1)} %get-tuple-element.12.down, bf16[2,4,256,2048]{3,2,1,0:T(8,128)(2,1)S(1)} %get-tuple-element.13.gate, ...), custom_call_target="tpu_custom_call" | custom-call | tf_op jit(solution)/shard_map/write/pallas_call | solution.py:406

commit v4 on v3

--- a/solution.py
+++ b/solution.py
@@ -139,6 +139,86 @@
     for s in swaps[:4]:
         s.start()
 
+    def piece(arr, t, c):
+        if arr == DOWN:
+            return down.at[c, k, pl.ds(16 * t, 16), :]
+        ref = gate if arr == GATE else up
+        return ref.at[k, t, :, pl.ds(pl.multiple_of(c * 128, 128), 128)]
+
+    def origin(t, a, b):
+        dx, dy = (a, b) if TREES[t][0] == "x" else (b, a)
+        return lax.rem(y - dy + 4, 4) * 4 + lax.rem(x - dx + 4, 4)
+
+    def way_to(t, a, b, na, nb):
+        first_axis, sign = TREES[t]
+        second_axis = "y" if first_axis == "x" else "x"
+        if na != a:
+            return first_axis, (-sign if na == -sign else sign)
+        return second_axis, (-sign if nb == -sign else sign)
+
+    def copy_on(arr, t, c, na, nb, to):
+        ref = piece(arr, t, c)
+        return pltpu.make_async_remote_copy(
+            src_ref=ref, dst_ref=ref, send_sem=send_sem.at[arr],
+            recv_sem=recv_sem.at[(arr * 4 + t) * 16 + slot_number(na, nb)],
+            device_id=to, device_id_type=MESH,
+        )
+
+    def send_on(arr, t, a, b, c, only=None):
+        for na, nb in onward(a, b, TREES[t][1]):
+            way = way_to(t, a, b, na, nb)
+            if only is None or way == only:
+                copy_on(arr, t, c, na, nb, toward(*way)).start()
+
+    def send_side(arr, t, c):
+        ref = piece(arr, t, c)
+        pltpu.make_async_remote_copy(
+            src_ref=ref, dst_ref=ref, send_sem=side_send.at[arr], recv_sem=side_recv.at[arr],
+            device_id=partner, device_id_type=MESH,
+        ).start()
+
+    def arrive(arr, t, a, b):
+        c = origin(t, a, b)
+        copy_on(arr, t, c, a, b, partner).wait_recv()
+        send_on(arr, t, a, b, c)
+        send_side(arr, t, c)
+
+    def row_copy(rows, w):
+        return pltpu.make_async_remote_copy(
+            src_ref=norm.at[rows], dst_ref=norm.at[rows], send_sem=n_send.at[w], recv_sem=n_recv.at[w],
+            device_id=toward(*WAYS[w]), device_id_type=MESH,
+        )
+
+    def row_from(w):
+        axis, by = WAYS[w]
+        if axis == "x":
+            return pl.ds(y * 4 + lax.rem(x - by + 4, 4), 1)
+        return pl.ds(lax.rem(y - by + 4, 4) * 4, 4)
+
+    for i in range(3):
+        reads[i].wait()
+    for t in range(4):
+        quarter = pl.ds(16 * t, 16)
+        mix = lax.dot_general(
+            hd[:, quarter], ld[...], (((0,), (0,)), ((), ())), preferred_element_type=jnp.float32
+        )
+        full = wd[quarter, :].astype(jnp.float32) + mix_rate * mix
+        down[chip, k, quarter, :] = full.astype(jnp.bfloat16)
+        for w in range(4):
+            @pl.when(jnp.logical_not(later(w)))
+            def _(t=t, w=w):
+                send_on(DOWN, t, 0, 0, chip, only=WAYS[w])
+
+    for w in range(4):
+        @pl.when(later(w))
+        def _(w=w):
+            pl.semaphore_wait(ready.at[w], 1)
+            for t in range(4):
+                send_on(DOWN, t, 0, 0, chip, only=WAYS[w])
+
+    for t in range(4):
+        send_side(DOWN, t, chip)
+
     reads[9].wait()
     reads[10].wait()
     lane = lax.broadcasted_iota(jnp.int32, (1, 128), 1)
@@ -148,88 +228,9 @@
         own = jnp.where(lane == first + i, train[i] + step[i], own)
     norm[chip] = own
 
-    for i in range(3):
-        reads[i].wait()
-    mix = lax.dot_general(hd[...], ld[...], (((0,), (0,)), ((), ())), preferred_element_type=jnp.float32)
-    down[chip, k] = (wd[...].astype(jnp.float32) + mix_rate * mix).astype(jnp.bfloat16)
-
-    def piece(arr, t, c):
-        if arr == DOWN:
-            return down.at[c, k, pl.ds(16 * t, 16), :]
-        ref = gate if arr == GATE else up
-        return ref.at[k, t, :, pl.ds(pl.multiple_of(c * 128, 128), 128)]
-
-    def origin(t, a, b):
-        dx, dy = (a, b) if TREES[t][0] == "x" else (b, a)
-        return lax.rem(y - dy + 4, 4) * 4 + lax.rem(x - dx + 4, 4)
-
-    def way_to(t, a, b, na, nb):
-        first_axis, sign = TREES[t]
-        second_axis = "y" if first_axis == "x" else "x"
-        if na != a:
-            return first_axis, (-sign if na == -sign else sign)
-        return second_axis, (-sign if nb == -sign else sign)
-
-    def copy_on(arr, t, c, na, nb, to):
-        ref = piece(arr, t, c)
-        return pltpu.make_async_remote_copy(
-            src_ref=ref, dst_ref=ref, send_sem=send_sem.at[arr],
-            recv_sem=recv_sem.at[(arr * 4 + t) * 16 + slot_number(na, nb)],
-            device_id=to, device_id_type=MESH,
-        )
-
-    def send_on(arr, t, a, b, c, only=None):
-        for na, nb in onward(a, b, TREES[t][1]):
-            way = way_to(t, a, b, na, nb)
-            if only is None or way == only:
-                copy_on(arr, t, c, na, nb, toward(*way)).start()
-
-    def send_side(arr, t, c):
-        ref = piece(arr, t, c)
-        pltpu.make_async_remote_copy(
-            src_ref=ref, dst_ref=ref, send_sem=side_send.at[arr], recv_sem=side_recv.at[arr],
-            device_id=partner, device_id_type=MESH,
-        ).start()
-
-    def arrive(arr, t, a, b):
-        c = origin(t, a, b)
-        copy_on(arr, t, c, a, b, partner).wait_recv()
-        send_on(arr, t, a, b, c)
-        send_side(arr, t, c)
-
-    def row_copy(rows, w):
-        return pltpu.make_async_remote_copy(
-            src_ref=norm.at[rows], dst_ref=norm.at[rows], send_sem=n_send.at[w], recv_sem=n_recv.at[w],
-            device_id=toward(*WAYS[w]), device_id_type=MESH,
-        )
-
-    def row_from(w):
-        axis, by = WAYS[w]
-        if axis == "x":
-            return pl.ds(y * 4 + lax.rem(x - by + 4, 4), 1)
-        return pl.ds(lax.rem(y - by + 4, 4) * 4, 4)
-
-    def first_sends(w):
-        if w < 2:
-            row_copy(pl.ds(chip, 1), w).start()
-        for t in range(4):
-            send_on(DOWN, t, 0, 0, chip, only=WAYS[w])
-
-    for w in range(4):
-        @pl.when(jnp.logical_not(later(w)))
-        def _(w=w):
-            first_sends(w)
-
-    for w in range(4):
-        @pl.when(later(w))
-        def _(w=w):
-            pl.semaphore_wait(ready.at[w], 1)
-            first_sends(w)
-
     wait_ready(4)
-    row_copy(pl.ds(chip, 1), 4).start()
-    for t in range(4):
-        send_side(DOWN, t, chip)
+    for w in (0, 1, 4):
+        row_copy(pl.ds(chip, 1), w).start()
 
     def turned(ref, w, low, high):
         for t in range(4):
@@ -347,19 +348,20 @@
     drain(UP, up.at[k, :, :, pl.ds(0, 1920)], up.at[other], up.at[k])
 
 
-def write_kernel(down, gate, up, norm, down_out, gate_out, up_out, norm_out, sem):
+def write_kernel(down, gate, up, norm, down_out, gate_out, up_out, norm_out, rounded, sem):
+    rounded[...] = norm[...].reshape(16, 128).astype(jnp.bfloat16)
     copies = []
-    for n, (src, dst) in enumerate([(gate, gate_out), (up, up_out)]):
+    for src, dst in ((gate, gate_out), (up, up_out)):
         for h in range(2):
             for t in range(4):
                 copies.append((src.at[h, t], dst.at[h, t]))
     for q in range(8):
         rows = pl.ds(2 * q, 2)
         copies.append((down.at[rows], down_out.at[rows]))
+    copies.append((rounded, norm_out))
     copies = [pltpu.make_async_copy(s, d, sem.at[i]) for i, (s, d) in enumerate(copies)]
     for c in copies:
         c.start()
-    norm_out[...] = norm[...].reshape(16, 128).astype(jnp.bfloat16)
     for c in copies:
         c.wait()
 
@@ -412,8 +414,8 @@
             jax.ShapeDtypeStruct((16, 128), bf16),
         ),
         in_specs=[vmem] * 4,
-        out_specs=(hbm, hbm, hbm, vmem),
-        scratch_shapes=[dma((24,))],
+        out_specs=(hbm,) * 4,
+        scratch_shapes=[pltpu.VMEM((16, 128), bf16), dma((25,))],
         compiler_params=pltpu.CompilerParams(vmem_limit_bytes=4 << 20),
         name="write",
     )(down, gate, up, norm)

time: 83.1 us -> 82.4 us (level)
  no operation moved by 1% of the time
where the time goes in v4:
time: 82.4 us; the launch traced here: 82.3 us
  Pallas kernels  81.6 us (99%)
    pallas_call x1, Pallas kernels, local(): pl.pallas_call(gather_kernel, out_shape=(pltpu.VMEM((16, 2, 64, 2048), bf...  73 us
    pallas_call x1, Pallas kernels, local(): pl.pallas_call(write_kernel, out_shape=(jax.ShapeDtypeStruct((16, 2, 64,...  8.57 us

profile of v4, /device:TPU:1, one launch (start us, length us, event | category | flops | bytes accessed | tf_op | source)
XLA Modules:
  0.0 82.3 jit_solution(2517417966425707760)
XLA Ops:
  0.6 73.0 %gather.1 = (bf16[16,2,64,2048]{3,2,1,0:T(8,128)(2,1)S(1)}, bf16[2,4,256,2048]{3,2,1,0:T(8,128)(2,1)S(1)}, bf16[2,4,256,2048]{3,2,1,0:T(8,128)(2,1)S(1)}, f32[16,1,128]{2,1,0:T(1,128)S(1)}) custom-call(bf16[64,2048]{1,0:T(8,128)(2,1)} %bitcast.6, bf16[64,2048]{1,0:T(8,128)(2,1)} %bitcast.7, bf16[64,64]{1,0:T(8,128)(2,1)} %hd_in.1, bf16[64,2048]{1,0:T(8,128)(2,1)} %wg_in.1, ...), custom_call_target="tpu_custom_call" | custom-call | tf_op jit(solution)/shard_map/gather/pallas_call | solution.py:378
  73.7 8.6 %write.1 = (bf16[16,2,64,2048]{3,2,1,0:T(8,128)(2,1)}, bf16[2,4,256,2048]{3,2,1,0:T(8,128)(2,1)}, bf16[2,4,256,2048]{3,2,1,0:T(8,128)(2,1)}, bf16[16,128]{1,0:T(8,128)(2,1)}) custom-call(bf16[16,2,64,2048]{3,2,1,0:T(8,128)(2,1)S(1)} %get-tuple-element.12.down, bf16[2,4,256,2048]{3,2,1,0:T(8,128)(2,1)S(1)} %get-tuple-element.13.gate, ...), custom_call_target="tpu_custom_call" | custom-call | tf_op jit(solution)/shard_map/write/pallas_call | solution.py:408

commit v5 on v4

--- a/solution.py
+++ b/solution.py
@@ -66,6 +66,18 @@
         return {"model": lax.rem(z + by + 4, 4)}
 
     partner = {"rows_2": other}
+
+    def later(way):
+        axis, by = WAYS[way]
+        p = place[axis]
+        return (p == 0) | (p == 3) if by == -1 else p < 2
+
+    barrier = pltpu.get_barrier_semaphore()
+    pl.semaphore_signal(barrier, inc=1, device_id=partner, device_id_type=MESH)
+    for w in range(6):
+        @pl.when(later(w))
+        def _(w=w):
+            pl.semaphore_signal(barrier, inc=1, device_id=toward(*WAYS[w]), device_id_type=MESH)
 
     half = pl.ds(pl.multiple_of(k * 1024, 1024), 1024)
     half_other = pl.ds(pl.multiple_of(other * 1024, 1024), 1024)
@@ -81,22 +93,10 @@
             ]
         )
     ]
-    for r in reads:
+    for r in reads[:3]:
         r.start()
     below[...] = jnp.zeros_like(below)
     above[...] = jnp.zeros_like(above)
-
-    def later(way):
-        axis, by = WAYS[way]
-        p = place[axis]
-        return (p == 0) | (p == 3) if by == -1 else p < 2
-
-    barrier = pltpu.get_barrier_semaphore()
-    pl.semaphore_signal(barrier, inc=1, device_id=partner, device_id_type=MESH)
-    for w in range(6):
-        @pl.when(later(w))
-        def _(w=w):
-            pl.semaphore_signal(barrier, inc=1, device_id=toward(*WAYS[w]), device_id_type=MESH)
 
     @pl.when(z < 3)
     def _():
@@ -114,6 +114,9 @@
                 ready.at[BACK[w]], inc=1, device_id=toward(*WAYS[w]), device_id_type=MESH
             )
 
+    for r in reads[3:]:
+        r.start()
+
     @pl.when(z > 0)
     def _():
         pl.semaphore_signal(ready.at[6], inc=1, device_id=toward("z", -1), device_id_type=MESH)
@@ -139,11 +142,11 @@
     for s in swaps[:4]:
         s.start()
 
-    def piece(arr, t, c):
+    def piece(arr, t, c, h):
         if arr == DOWN:
-            return down.at[c, k, pl.ds(16 * t, 16), :]
+            return down.at[c, h, pl.ds(16 * t, 16), :]
         ref = gate if arr == GATE else up
-        return ref.at[k, t, :, pl.ds(pl.multiple_of(c * 128, 128), 128)]
+        return ref.at[h, t, :, pl.ds(pl.multiple_of(c * 128, 128), 128)]
 
     def origin(t, a, b):
         dx, dy = (a, b) if TREES[t][0] == "x" else (b, a)
@@ -156,11 +159,14 @@
             return first_axis, (-sign if na == -sign else sign)
         return second_axis, (-sign if nb == -sign else sign)
 
-    def copy_on(arr, t, c, na, nb, to):
-        ref = piece(arr, t, c)
+    def copy_on(arr, t, c, na, nb, to, h):
+        ref = piece(arr, t, c, h)
+        number = slot_number(na, nb)
+        if abs(na) + abs(nb) == 4:
+            to, number = {**to, "rows_2": 1}, number * h
         return pltpu.make_async_remote_copy(
             src_ref=ref, dst_ref=ref, send_sem=send_sem.at[arr],
-            recv_sem=recv_sem.at[(arr * 4 + t) * 16 + slot_number(na, nb)],
+            recv_sem=recv_sem.at[(arr * 4 + t) * 16 + number],
             device_id=to, device_id_type=MESH,
         )
 
@@ -168,20 +174,28 @@
         for na, nb in onward(a, b, TREES[t][1]):
             way = way_to(t, a, b, na, nb)
             if only is None or way == only:
-                copy_on(arr, t, c, na, nb, toward(*way)).start()
-
-    def send_side(arr, t, c):
-        ref = piece(arr, t, c)
+                copy_on(arr, t, c, na, nb, toward(*way), k).start()
+
+    def send_side(arr, t, c, h=None):
+        ref = piece(arr, t, c, k if h is None else h)
+        sem = arr if h is None else 3 + arr
         pltpu.make_async_remote_copy(
-            src_ref=ref, dst_ref=ref, send_sem=side_send.at[arr], recv_sem=side_recv.at[arr],
+            src_ref=ref, dst_ref=ref, send_sem=side_send.at[sem], recv_sem=side_recv.at[sem],
             device_id=partner, device_id_type=MESH,
         ).start()
 
     def arrive(arr, t, a, b):
         c = origin(t, a, b)
-        copy_on(arr, t, c, a, b, partner).wait_recv()
+        copy_on(arr, t, c, a, b, partner, k).wait_recv()
         send_on(arr, t, a, b, c)
         send_side(arr, t, c)
+
+    def arrive_last(arr, t, a, b):
+        c = origin(t, a, b)
+        copy_on(arr, t, c, a, b, {}, 1).wait_recv()
+        send_side(arr, t, c)
+        copy_on(arr, t, c, a, b, {}, 0).wait_recv()
+        send_side(arr, t, c, 0)
 
     def row_copy(rows, w):
         return pltpu.make_async_remote_copy(
@@ -328,7 +342,7 @@
             for arr in (DOWN, GATE, UP) for a, b in places for t in range(4)
         ]
 
-    events = [e for hops in (1, 2, 3, 4) for e in level(hops)]
+    events = [e for hops in (1, 2, 3) for e in level(hops)]
     extra = {
         0: rows_along_y, 48: rows_to_partner, 60: rows_of_chip, 72: z_ends,
         96: z_up_sum, 108: z_up_send, 120: z_down_sum, 132: z_down_send, 150: norm_end,
@@ -338,18 +352,42 @@
             extra[n]()
         arrive(*e)
 
-    def drain(arr, sent, other_half, own_half):
-        pltpu.make_async_copy(sent, sent, send_sem.at[arr]).wait()
-        pltpu.make_async_copy(own_half, own_half, side_send.at[arr]).wait()
-        pltpu.make_async_copy(other_half, other_half, side_recv.at[arr]).wait()
-
-    drain(DOWN, down.at[pl.ds(0, 15), k], down.at[:, other], down.at[:, k])
-    drain(GATE, gate.at[k, :, :, pl.ds(0, 1920)], gate.at[other], gate.at[k])
-    drain(UP, up.at[k, :, :, pl.ds(0, 1920)], up.at[other], up.at[k])
+    @pl.when(k == 1)
+    def _():
+        for e in level(4):
+            arrive_last(*e)
+
+    def wait_for(ref, sem):
+        pltpu.make_async_copy(ref, ref, sem).wait()
+
+    def most(arr, h):
+        if arr == DOWN:
+            return down.at[pl.ds(0, 15), h]
+        return (gate if arr == GATE else up).at[h, :, :, pl.ds(0, 1920)]
+
+    def whole(arr, h):
+        return down.at[:, h] if arr == DOWN else (gate if arr == GATE else up).at[h]
+
+    last = down.at[0, 0]
+    for arr in (DOWN, GATE, UP):
+        wait_for(most(arr, k), send_sem.at[arr])
+
+    @pl.when(k == 1)
+    def _():
+        for arr in (DOWN, GATE, UP):
+            wait_for(most(arr, 0), side_recv.at[arr])
+            wait_for(whole(arr, 1), side_send.at[arr])
+            wait_for(last, side_send.at[3 + arr])
+
+    @pl.when(k == 0)
+    def _():
+        for arr in (DOWN, GATE, UP):
+            wait_for(most(arr, 0), side_send.at[arr])
+            wait_for(whole(arr, 1), side_recv.at[arr])
+            wait_for(last, side_recv.at[3 + arr])
 
 
 def write_kernel(down, gate, up, norm, down_out, gate_out, up_out, norm_out, rounded, sem):
-    rounded[...] = norm[...].reshape(16, 128).astype(jnp.bfloat16)
     copies = []
     for src, dst in ((gate, gate_out), (up, up_out)):
         for h in range(2):
@@ -360,8 +398,10 @@
         copies.append((down.at[rows], down_out.at[rows]))
     copies.append((rounded, norm_out))
     copies = [pltpu.make_async_copy(s, d, sem.at[i]) for i, (s, d) in enumerate(copies)]
-    for c in copies:
+    for c in copies[:-1]:
         c.start()
+    rounded[...] = norm[...].reshape(16, 128).astype(jnp.bfloat16)
+    copies[-1].start()
     for c in copies:
         c.wait()
 
@@ -391,7 +431,7 @@
             pltpu.VMEM((128, 1024), bf16), pltpu.VMEM((128, 64), bf16), pltpu.VMEM((64, 1024), bf16),
             pltpu.SMEM((16,), f32), pltpu.SMEM((16,), f32),
             rows, rows, rows, rows, rows, pltpu.VMEM((2, 16, 1, 128), f32),
-            dma((11,)), dma((5,)), dma((5,)), dma((3,)), dma((3,)), dma((3,)), dma((192,)),
+            dma((11,)), dma((5,)), dma((5,)), dma((3,)), dma((6,)), dma((6,)), dma((192,)),
             dma((8,)), dma((8,)), pltpu.SemaphoreType.REGULAR((7,)),
         ],
         compiler_params=pltpu.CompilerParams(

time: 82.4 us -> 82.3 us (level)
  no operation moved by 1% of the time
where the time goes in v5:
time: 82.3 us; the launch traced here: 82.1 us
  Pallas kernels  81.5 us (99%)
    pallas_call x1, Pallas kernels, local(): pl.pallas_call(gather_kernel, out_shape=(pltpu.VMEM((16, 2, 64, 2048), bf...  72.9 us
    pallas_call x1, Pallas kernels, local(): pl.pallas_call(write_kernel, out_shape=(jax.ShapeDtypeStruct((16, 2, 64,...  8.57 us

profile of v5, /device:TPU:1, one launch (start us, length us, event | category | flops | bytes accessed | tf_op | source)
XLA Modules:
  0.0 82.1 jit_solution(11140129206194900229)
XLA Ops:
  0.6 72.9 %gather.1 = (bf16[16,2,64,2048]{3,2,1,0:T(8,128)(2,1)S(1)}, bf16[2,4,256,2048]{3,2,1,0:T(8,128)(2,1)S(1)}, bf16[2,4,256,2048]{3,2,1,0:T(8,128)(2,1)S(1)}, f32[16,1,128]{2,1,0:T(1,128)S(1)}) custom-call(bf16[64,2048]{1,0:T(8,128)(2,1)} %bitcast.6, bf16[64,2048]{1,0:T(8,128)(2,1)} %bitcast.7, bf16[64,64]{1,0:T(8,128)(2,1)} %hd_in.1, bf16[64,2048]{1,0:T(8,128)(2,1)} %wg_in.1, ...), custom_call_target="tpu_custom_call" | custom-call | tf_op jit(solution)/shard_map/gather/pallas_call | solution.py:418
  73.6 8.6 %write.1 = (bf16[16,2,64,2048]{3,2,1,0:T(8,128)(2,1)}, bf16[2,4,256,2048]{3,2,1,0:T(8,128)(2,1)}, bf16[2,4,256,2048]{3,2,1,0:T(8,128)(2,1)}, bf16[16,128]{1,0:T(8,128)(2,1)}) custom-call(bf16[16,2,64,2048]{3,2,1,0:T(8,128)(2,1)S(1)} %get-tuple-element.12.down, bf16[2,4,256,2048]{3,2,1,0:T(8,128)(2,1)S(1)} %get-tuple-element.13.gate, ...), custom_call_target="tpu_custom_call" | custom-call | tf_op jit(solution)/shard_map/write/pallas_call | solution.py:448

commit v6 on v4

--- a/solution.py
+++ b/solution.py
@@ -66,6 +66,18 @@
         return {"model": lax.rem(z + by + 4, 4)}
 
     partner = {"rows_2": other}
+
+    def later(way):
+        axis, by = WAYS[way]
+        p = place[axis]
+        return (p == 0) | (p == 3) if by == -1 else p < 2
+
+    barrier = pltpu.get_barrier_semaphore()
+    pl.semaphore_signal(barrier, inc=1, device_id=partner, device_id_type=MESH)
+    for w in range(6):
+        @pl.when(later(w))
+        def _(w=w):
+            pl.semaphore_signal(barrier, inc=1, device_id=toward(*WAYS[w]), device_id_type=MESH)
 
     half = pl.ds(pl.multiple_of(k * 1024, 1024), 1024)
     half_other = pl.ds(pl.multiple_of(other * 1024, 1024), 1024)
@@ -81,22 +93,10 @@
             ]
         )
     ]
-    for r in reads:
+    for r in reads[:3]:
         r.start()
     below[...] = jnp.zeros_like(below)
     above[...] = jnp.zeros_like(above)
-
-    def later(way):
-        axis, by = WAYS[way]
-        p = place[axis]
-        return (p == 0) | (p == 3) if by == -1 else p < 2
-
-    barrier = pltpu.get_barrier_semaphore()
-    pl.semaphore_signal(barrier, inc=1, device_id=partner, device_id_type=MESH)
-    for w in range(6):
-        @pl.when(later(w))
-        def _(w=w):
-            pl.semaphore_signal(barrier, inc=1, device_id=toward(*WAYS[w]), device_id_type=MESH)
 
     @pl.when(z < 3)
     def _():
@@ -114,6 +114,9 @@
                 ready.at[BACK[w]], inc=1, device_id=toward(*WAYS[w]), device_id_type=MESH
             )
 
+    for r in reads[3:]:
+        r.start()
+
     @pl.when(z > 0)
     def _():
         pl.semaphore_signal(ready.at[6], inc=1, device_id=toward("z", -1), device_id_type=MESH)
@@ -180,8 +183,8 @@
     def arrive(arr, t, a, b):
         c = origin(t, a, b)
         copy_on(arr, t, c, a, b, partner).wait_recv()
+        send_side(arr, t, c)
         send_on(arr, t, a, b, c)
-        send_side(arr, t, c)
 
     def row_copy(rows, w):
         return pltpu.make_async_remote_copy(
@@ -215,9 +218,6 @@
             pl.semaphore_wait(ready.at[w], 1)
             for t in range(4):
                 send_on(DOWN, t, 0, 0, chip, only=WAYS[w])
-
-    for t in range(4):
-        send_side(DOWN, t, chip)
 
     reads[9].wait()
     reads[10].wait()
@@ -247,7 +247,6 @@
         turned(ref, *args)
         for t in range(4):
             send_on(arr, t, 0, 0, chip)
-            send_side(arr, t, chip)
 
     def rows_along_y():
         for w in (0, 1, 4):
@@ -257,6 +256,9 @@
             row_copy(pl.ds(y * 4, 4), w).start()
 
     def rows_to_partner():
+        for arr in (DOWN, GATE, UP):
+            for t in range(4):
+                send_side(arr, t, chip)
         for w in (2, 3, 5):
             row_copy(row_from(w), w).wait_recv()
         swaps[4].start()
@@ -349,7 +351,6 @@
 
 
 def write_kernel(down, gate, up, norm, down_out, gate_out, up_out, norm_out, rounded, sem):
-    rounded[...] = norm[...].reshape(16, 128).astype(jnp.bfloat16)
     copies = []
     for src, dst in ((gate, gate_out), (up, up_out)):
         for h in range(2):
@@ -360,8 +361,10 @@
         copies.append((down.at[rows], down_out.at[rows]))
     copies.append((rounded, norm_out))
     copies = [pltpu.make_async_copy(s, d, sem.at[i]) for i, (s, d) in enumerate(copies)]
-    for c in copies:
+    for c in copies[:-1]:
         c.start()
+    rounded[...] = norm[...].reshape(16, 128).astype(jnp.bfloat16)
+    copies[-1].start()
     for c in copies:
         c.wait()
 

time: 82.4 us -> 82.4 us (level)
  no operation moved by 1% of the time
where the time goes in v6:
time: 82.4 us; the launch traced here: 82.3 us
  Pallas kernels  81.7 us (99%)
    pallas_call x1, Pallas kernels, local(): pl.pallas_call(gather_kernel, out_shape=(pltpu.VMEM((16, 2, 64, 2048), bf...  73.1 us
    pallas_call x1, Pallas kernels, local(): pl.pallas_call(write_kernel, out_shape=(jax.ShapeDtypeStruct((16, 2, 64,...  8.57 us

profile of v6, /device:TPU:1, one launch (start us, length us, event | category | flops | bytes accessed | tf_op | source)
XLA Modules:
  0.0 82.3 jit_solution(39012146032103138)
XLA Ops:
  0.6 73.1 %gather.1 = (bf16[16,2,64,2048]{3,2,1,0:T(8,128)(2,1)S(1)}, bf16[2,4,256,2048]{3,2,1,0:T(8,128)(2,1)S(1)}, bf16[2,4,256,2048]{3,2,1,0:T(8,128)(2,1)S(1)}, f32[16,1,128]{2,1,0:T(1,128)S(1)}) custom-call(bf16[64,2048]{1,0:T(8,128)(2,1)} %bitcast.6, bf16[64,2048]{1,0:T(8,128)(2,1)} %bitcast.7, bf16[64,64]{1,0:T(8,128)(2,1)} %hd_in.1, bf16[64,2048]{1,0:T(8,128)(2,1)} %wg_in.1, ...), custom_call_target="tpu_custom_call" | custom-call | tf_op jit(solution)/shard_map/gather/pallas_call | solution.py:381
  73.7 8.6 %write.1 = (bf16[16,2,64,2048]{3,2,1,0:T(8,128)(2,1)}, bf16[2,4,256,2048]{3,2,1,0:T(8,128)(2,1)}, bf16[2,4,256,2048]{3,2,1,0:T(8,128)(2,1)}, bf16[16,128]{1,0:T(8,128)(2,1)}) custom-call(bf16[16,2,64,2048]{3,2,1,0:T(8,128)(2,1)S(1)} %get-tuple-element.12.down, bf16[2,4,256,2048]{3,2,1,0:T(8,128)(2,1)S(1)} %get-tuple-element.13.gate, ...), custom_call_target="tpu_custom_call" | custom-call | tf_op jit(solution)/shard_map/write/pallas_call | solution.py:411
